TPU v7x, 512 devices: a whole 4x8x8 slice. The times are simulated.
512 devices in a mesh: fsdp: 64 (over x, y, core), dp: 8 (over z).
Axes of the slice: x: 4, y: 8, z: 8, core: 2. Of those that a mesh axis runs over, the one named last changes fastest.
Arguments:
- grads: bfloat16 [8, 1024, 28672], P('dp', 'fsdp')
- block_slot: int32 [28], replicated, may hold values from 0 to 63, as said below
- left_stats: float32 [64, 1024, 1024], P('fsdp', 'dp')
- right_stats: float32 [64, 1024, 1024], P('fsdp', 'dp')
- left_root: bfloat16 [64, 1024, 1024], P('fsdp', 'dp')
- right_root: bfloat16 [64, 1024, 1024], P('fsdp', 'dp')
Outputs:
- left_new: float32 [64, 1024, 1024], P('fsdp', 'dp')
- right_new: float32 [64, 1024, 1024], P('fsdp', 'dp')
- update: bfloat16 [1024, 28672], P('fsdp')
Inputs may be any that keep to these rules, and one draw needn't show every extreme that they name: The entries of block_slot are distinct. Block b's statistics and roots sit in slot block_slot[b], which belongs to the fsdp device of index block_slot[b]; slots that no block names are empty and their statistics pass through unchanged.
All inputs are finite; a program needn't handle non-finite values.
Results may differ from a plain program's by a relative error of at most 0.015.
Values may be sent and summed in bfloat16 or wider, within the bound.
No kernel may reach another device: no remote copies, remote signals or barrier semaphores. Data moves between devices by JAX's collectives and lax.ppermute only.
A program may use at most 64 MiB of HBM per device.

v0:
```python
import jax
import jax.numpy as jnp
from jax import lax
from jax.sharding import Mesh
from jax.sharding import PartitionSpec as P

FSDP = ("fsdp_0", "fsdp_1", "fsdp_2")
epsilon = 1e-06


def per_device(grads, block_slot, left_stats, right_stats, left_root, right_root):
    rows = grads[0]
    row_dev, col_count = rows.shape
    block_size = left_stats.shape[2]
    block_count = col_count // block_size
    shared = left_stats.shape[1]
    replicas = lax.axis_size("dp")
    total_slots = lax.axis_size(FSDP)
    slot_ids = jnp.arange(total_slots, dtype=jnp.int32)
    matches = block_slot[None, :] == slot_ids[:, None]
    filled = jnp.any(matches, axis=1)
    numbers = jnp.arange(block_count, dtype=jnp.int32)
    source = jnp.sum(jnp.where(matches, numbers[None, :], 0), axis=1)
    whole_left = lax.all_gather(left_root[0], "dp", axis=0, tiled=True)
    shares = rows.reshape(row_dev, block_count, replicas, shared).transpose(2, 1, 0, 3)
    shares = shares.reshape(replicas, block_count * row_dev, shared)
    roots = right_root[0].reshape(shared, replicas, shared).transpose(1, 0, 2)
    message = jnp.concatenate([shares, roots], axis=1)
    received = lax.all_to_all(message, "dp", 0, 0, tiled=True)
    summed = jnp.sum(received[:, : block_count * row_dev].astype(jnp.float32), axis=0)
    summed = summed.astype(jnp.bfloat16).reshape(block_count, row_dev, shared)
    right_cols = received[:, block_count * row_dev :]
    outgoing = jnp.where(
        filled[:, None, None], jnp.take(summed, source, axis=0), jnp.zeros((), jnp.bfloat16)
    )
    incoming = lax.all_to_all(outgoing, FSDP, 0, 0, tiled=True)
    mine, whole_left = lax.optimization_barrier((incoming.reshape(block_size, shared), whole_left))
    gradient = lax.all_gather(mine, "dp", axis=1, tiled=True)
    inner = jnp.einsum(
        "rk,kc->rc",
        gradient,
        right_cols.reshape(block_size, shared),
        preferred_element_type=jnp.float32,
    )
    high = lax.reduce_precision(inner, 8, 7)
    low = (inner - high).astype(jnp.bfloat16)
    high = high.astype(jnp.bfloat16)
    both = jnp.einsum(
        "kr,rc->kc", whole_left, high, preferred_element_type=jnp.float32
    ) + jnp.einsum("kr,rc->kc", whole_left, low, preferred_element_type=jnp.float32)
    both = both.astype(jnp.bfloat16).reshape(total_slots, row_dev, shared)
    back = lax.all_to_all(both, FSDP, 0, 0, tiled=True)
    row_start = lax.axis_index("dp") * shared
    own_rows = lax.dynamic_slice_in_dim(gradient, row_start, shared, 0)
    left_new = left_stats + jnp.einsum(
        "rc,kc->rk", own_rows, gradient, preferred_element_type=jnp.float32
    )
    right_new = right_stats + jnp.einsum(
        "rc,rk->ck", mine, gradient, preferred_element_type=jnp.float32
    )
    wide = back.astype(jnp.float32)
    squares = lax.psum(jnp.sum(wide * wide, axis=(1, 2)), FSDP + ("dp",))
    picked = jnp.take(back, block_slot, axis=0)
    full = lax.all_gather(picked, "dp", axis=0, tiled=False)
    factor = lax.rsqrt(jnp.take(squares, block_slot) / (block_size * block_size) + epsilon)
    update = (full.astype(jnp.float32) * factor[None, :, None, None]).astype(jnp.bfloat16)
    update = update.transpose(2, 1, 0, 3).reshape(row_dev, col_count)
    return (left_new, right_new, update)


def solution(mesh):
    split = Mesh(
        mesh.devices.reshape(4, 8, 2, mesh.shape["dp"]), ("fsdp_0", "fsdp_1", "fsdp_2", "dp")
    )
    placed = (
        P("dp", FSDP, None),
        P(),
        P(FSDP, "dp", None),
        P(FSDP, "dp", None),
        P(FSDP, "dp", None),
        P(FSDP, "dp", None),
    )
    return jax.shard_map(
        per_device,
        mesh=split,
        in_specs=placed,
        out_specs=(P(FSDP, "dp", None), P(FSDP, "dp", None), P(FSDP, None)),
        check_vma=False,
    )
```

profile of v0, /device:TPU:2, one launch (start us, length us, event | category | flops | bytes accessed | tf_op | source)
XLA Modules:
  0.0 291.5 jit_solution(8681560645915231170)
XLA Ops:
  7.2 0.0 all-gather.6.cloned.1.call-start
  7.2 0.7 all-gather.6.cloned.1.call-update
  7.9 1.1 copy.24
  9.0 0.2 copy.25
  9.2 1.3 copy.27
  10.5 0.4 copy.23
  10.9 0.0 copy-start.6
  10.9 1.1 pad_maximum_fusion
  12.0 10.3 %all-to-all-start = ((bf16[8,576,128]{2,1,0:T(8,128)(2,1)}), bf16[8,576,128]{2,1,0:T(8,128)(2,1)S(1)}, u32[]{:S(2)}, u32[]{:S(2)}) async-start(bf16[8,576,128]{2,1,0:T(8,128)(2,1)} %pad_maximum_fusion), calls=%async_computation | async-start | bytes 2359296 | tf_op jit(solution)/shard_map/all_to_all | solution.py:29
  22.3 0.0 all-gather.4.cloned.1.call-start
  22.4 0.0 copy-done.6
  22.4 0.1 select_reduce_fusion
  22.5 0.1 fusion.8
  22.6 41.9 %all-to-all-done = bf16[8,576,128]{2,1,0:T(8,128)(2,1)S(1)} async-done(((bf16[8,576,128]{2,1,0:T(8,128)(2,1)}), bf16[8,576,128]{2,1,0:T(8,128)(2,1)S(1)}, u32[]{:S(2)}, u32[]{:S(2)}) %all-to-all-start) | async-done | bytes 1179680 | tf_op jit(solution)/shard_map/all_to_all | solution.py:29
  64.5 0.1 slice_reduce_fusion
  64.6 0.6 gather_fusion
  65.3 0.2 select_select_fusion
  65.5 22.4 %all_to_all.15 = bf16[64,16,128]{2,1,0:T(8,128)(2,1)} all-to-all(bf16[64,16,128]{2,1,0:T(8,128)(2,1)S(1)} %select_select_fusion), channel_id=1, replica_groups=mesh['fsdp_0'=4,'fsdp_1'=8,'fsdp_2'=2,'dp'=8] {'fsdp_0','fsdp_1','fsdp_2'}, dimensions={0} | all-to-all | bytes 524288 | tf_op jit(solution)/shard_map/all_to_all | solution.py:36
  87.9 0.0 all-gather.6.cloned.1.call-done
  87.9 0.0 copy-start.1
  87.9 0.0 all-gather.4.cloned.1.call-update
  88.0 42.8 %all-gather.4.cloned.1.call-done = bf16[1024,1024]{1,0:T(8,128)(2,1)} async-done(((bf16[1024,128]{1,0:T(8,128)(2,1)}), bf16[1024,1024]{1,0:T(8,128)(2,1)}) %all-gather.4.cloned.1.call-update) | async-done | bytes 2097168 | tf_op jit(solution)/shard_map/all_gather | solution.py:38
  130.7 2.3 fusion.11
  133.0 0.0 copy-done.1
  133.0 0.0 copy-start.2
  133.0 0.7 fusion.6
  133.8 0.9 copy-done.2
  134.6 0.0 copy-start
  134.6 0.0 copy-start.4
  134.6 1.4 fusion.2
  136.1 10.4 %all-to-all-start.2 = ((bf16[64,16,128]{2,1,0:T(8,128)(2,1)}), bf16[64,16,128]{2,1,0:T(8,128)(2,1)S(1)}, u32[]{:S(2)}, u32[]{:S(2)}) async-start(bf16[64,16,128]{2,1,0:T(8,128)(2,1)} %bitcast.12), calls=%async_computation.2 | async-start | bytes 524288 | tf_op jit(solution)/shard_map/all_to_all | solution.py:52
  146.5 0.0 copy-done
  146.5 0.0 copy-done.4
  146.5 0.0 copy-start.5
  146.5 1.6 fusion
  148.1 0.0 copy-done.3
  148.1 0.0 copy-done.5
  148.1 1.3 fusion.1
  149.4 8.6 %all-to-all-done.2 = bf16[64,16,128]{2,1,0:T(8,128)(2,1)S(1)} async-done(((bf16[64,16,128]{2,1,0:T(8,128)(2,1)}), bf16[64,16,128]{2,1,0:T(8,128)(2,1)S(1)}, u32[]{:S(2)}, u32[]{:S(2)}) %all-to-all-start.2) | async-done | bytes 262176 | tf_op jit(solution)/shard_map/all_to_all | solution.py:52
  158.0 0.6 multiply_reduce_fusion
  158.6 96.1 %psum.7 = f32[64]{0:T(128)S(1)} all-reduce(f32[64]{0:T(128)S(1)} %multiply_reduce_fusion), channel_id=1, replica_groups=mesh['fsdp_0'=4,'fsdp_1'=8,'fsdp_2'=2,'dp'=8] {'fsdp_0','fsdp_1','fsdp_2..., use_global_device_ids=true, to_apply=%region_4.5 | all-reduce | flops 64 | bytes 512 | tf_op jit(solution)/shard_map/psum | solution.py:62
  254.6 0.7 gather_fusion.2
  255.3 0.6 gather_fusion.1
  255.9 0.1 bitcast_select_fusion
  256.0 26.4 %all_gather.12 = bf16[8,28,16,128]{3,2,1,0:T(8,128)(2,1)S(1)} all-gather(bf16[1,28,16,128]{3,2,1,0:T(8,128)(2,1)S(1)} %bitcast_select_fusion), channel_id=1, replica_groups=mesh['fsdp_0'=4,'fsdp_1'=8,'fsdp_2'=2,'dp'=8] {'dp'}, dimensions={0}, use_global_device_ids=true | all-gather | bytes 1032192 | tf_op jit(solution)/shard_map/all_gather | solution.py:64
  282.5 0.3 fusion.3
  282.8 0.6 copy.26
  283.4 1.3 copy.30
  (8 shorter events, 0.1 us)
Async XLA Ops:
  7.2 80.7 %all-gather.6.cloned.1.call-start = ((), (), s32[]{:S(2)}) async-start(), calls=%async_computation.4 | async-start | bytes 2359296 | tf_op jit(solution)/shard_map/all_gather | solution.py:24
  10.9 11.5 %copy-start.6 = (s32[28]{0:T(128)S(1)}, s32[28]{0:T(128)}, u32[]{:S(2)}) copy-start(s32[28]{0:T(128)} %param.7) | copy-start | bytes 340
  12.0 52.5 %all-to-all-start = ((bf16[8,576,128]{2,1,0:T(8,128)(2,1)}), bf16[8,576,128]{2,1,0:T(8,128)(2,1)S(1)}, u32[]{:S(2)}, u32[]{:S(2)}) async-start(bf16[8,576,128]{2,1,0:T(8,128)(2,1)} %pad_maximum_fusion), calls=%async_computation | async-start | bytes 2359296 | tf_op jit(solution)/shard_map/all_to_all | solution.py:29
  22.3 108.4 %all-gather.4.cloned.1.call-start = ((), (), s32[]{:S(2)}) async-start(), calls=%async_computation.3 | async-start | bytes 2359296 | tf_op jit(solution)/shard_map/all_gather | solution.py:38
  87.9 45.1 %copy-start.1 = (bf16[1,1024,1024]{2,1,0:T(8,128)(2,1)S(1)}, bf16[1,1024,1024]{2,1,0:T(8,128)(2,1)}, u32[]{:S(2)}) copy-start(bf16[1,1024,1024]{2,1,0:T(8,128)(2,1)} %all-gather.6.cloned.1.call-done) | copy-start | bytes 6291460
  133.0 1.6 copy-start.2
  134.6 11.8 %copy-start = (bf16[1024,1024]{1,0:T(8,128)(2,1)S(1)}, bf16[1024,1024]{1,0:T(8,128)(2,1)}, u32[]{:S(2)}) copy-start(bf16[1024,1024]{1,0:T(8,128)(2,1)} %all-gather.4.cloned.1.call-done) | copy-start | bytes 6291460
  134.6 11.9 %copy-start.4 = (f32[1,128,1024]{2,1,0:T(8,128)S(1)}, f32[1,128,1024]{2,1,0:T(8,128)}, u32[]{:S(2)}) copy-start(f32[1,128,1024]{2,1,0:T(8,128)} %param.8) | copy-start | bytes 1572868
  136.1 12.1 %copy-start.3 = (bf16[64,16,128]{2,1,0:T(8,128)(2,1)S(1)}, bf16[64,16,128]{2,1,0:T(8,128)(2,1)}, u32[]{:S(2)}) copy-start(bf16[64,16,128]{2,1,0:T(8,128)(2,1)} %all_to_all.15) | copy-start | bytes 786436
  136.1 21.9 %all-to-all-start.2 = ((bf16[64,16,128]{2,1,0:T(8,128)(2,1)}), bf16[64,16,128]{2,1,0:T(8,128)(2,1)S(1)}, u32[]{:S(2)}, u32[]{:S(2)}) async-start(bf16[64,16,128]{2,1,0:T(8,128)(2,1)} %bitcast.12), calls=%async_computation.2 | async-start | bytes 524288 | tf_op jit(solution)/shard_map/all_to_all | solution.py:52
  146.5 1.7 copy-start.5
Sparse Core Ops, SparseCore 0:
  10.1 64.5 all-gather.5
  88.0 42.6 all-gather.3
where the time goes:
time: 292 us; the launch traced here: 291 us
  blocking collectives  145 us (50%)
  waiting for transfers between devices  94 us (32%)
  starting transfers between devices  20.8 us (7%)
  between operations  14.2 us (5%)
  local copies, waits for them, and re-layouts  7.68 us (3%)
  matrix products  7.32 us (3%)
    psum x1, blocking collectives, per_device(): squares = lax.psum(jnp.sum(wide * wide, axis=(1, 2)), FSDP + ('dp',))  96.1 us
    all_gather x1, waiting for transfers between devices, per_device(): gradient = lax.all_gather(mine, 'dp', axis=1, tiled=True)  42.8 us
    all_to_all x1, waiting for transfers between devices, per_device(): received = lax.all_to_all(message, 'dp', 0, 0, tiled=True)  41.9 us
    all_gather x1, blocking collectives, per_device(): full = lax.all_gather(picked, 'dp', axis=0, tiled=False)  26.4 us
    all_to_all x1, blocking collectives, per_device(): incoming = lax.all_to_all(outgoing, FSDP, 0, 0, tiled=True)  22.4 us
    all_to_all x1, starting transfers between devices, per_device(): back = lax.all_to_all(both, FSDP, 0, 0, tiled=True)  10.4 us
    all_to_all x1, starting transfers between devices, per_device(): received = lax.all_to_all(message, 'dp', 0, 0, tiled=True)  10.3 us
    all_to_all x1, waiting for transfers between devices, per_device(): back = lax.all_to_all(both, FSDP, 0, 0, tiled=True)  8.59 us
  transfers between devices with their start and end apart: 4, of which 3 were waited for; matrix products, arithmetic and copies ran while one was open for 3% of the time, Pallas kernels for 0%

commit v1 on v0

--- a/solution.py
+++ b/solution.py
@@ -35,7 +35,8 @@
     )
     incoming = lax.all_to_all(outgoing, FSDP, 0, 0, tiled=True)
     mine, whole_left = lax.optimization_barrier((incoming.reshape(block_size, shared), whole_left))
-    gradient = lax.all_gather(mine, "dp", axis=1, tiled=True)
+    sent = jnp.stack([mine] * lax.axis_size("dp"))
+    gradient = jnp.concatenate(lax.all_to_all(sent, "dp", 0, 0), axis=1)
     inner = jnp.einsum(
         "rk,kc->rc",
         gradient,

time: 292 us -> 298 us (1.021)
  waiting for transfers between devices: 94 us -> 97.5 us
  local copies, waits for them, and re-layouts: 7.68 us -> 10.9 us
    all_to_all x0 -> x1, waiting for transfers between devices: none -> 51.7 us  [per_device(): gradient = jnp.concatenate(lax.all_to_all(sent, 'dp', 0, 0), axis=1)]
    all_gather x1 -> x0, waiting for transfers between devices: 42.8 us -> none  [per_device(): gradient = lax.all_gather(mine, 'dp', axis=1, tiled=True)]
    all_to_all x1, waiting for transfers between devices: 8.59 us -> 4.15 us  [per_device(): back = lax.all_to_all(both, FSDP, 0, 0, tiled=True)]
    all_to_all x1, starting transfers between devices: 10.4 us -> 6.3 us  [per_device(): back = lax.all_to_all(both, FSDP, 0, 0, tiled=True)]
    all_to_all x0 -> x1, starting transfers between devices: none -> 3.6 us  [per_device(): gradient = jnp.concatenate(lax.all_to_all(sent, 'dp', 0, 0), axis=1)]
  transfers between devices with their start and end apart: 4 -> 4, of which waited for: 3 -> 3; matrix products, arithmetic and copies ran while one was open for 3% -> 4% of each run, Pallas kernels for 0% -> 0%
where the time goes in v1:
time: 298 us; the launch traced here: 297 us
  blocking collectives  144 us (48%)
  waiting for transfers between devices  97.5 us (33%)
  starting transfers between devices  20.3 us (7%)
  between operations  14.2 us (5%)
  local copies, waits for them, and re-layouts  10.9 us (4%)
  matrix products  7.57 us (3%)
    psum x1, blocking collectives, per_device(): squares = lax.psum(jnp.sum(wide * wide, axis=(1, 2)), FSDP + ('dp',))  95.3 us
    all_to_all x1, waiting for transfers between devices, per_device(): gradient = jnp.concatenate(lax.all_to_all(sent, 'dp', 0, 0), axis=1)  51.7 us
    all_to_all x1, waiting for transfers between devices, per_device(): received = lax.all_to_all(message, 'dp', 0, 0, tiled=True)  41 us
    all_gather x1, blocking collectives, per_device(): full = lax.all_gather(picked, 'dp', axis=0, tiled=False)  26.6 us
    all_to_all x1, blocking collectives, per_device(): incoming = lax.all_to_all(outgoing, FSDP, 0, 0, tiled=True)  22.2 us
    all_to_all x1, starting transfers between devices, per_device(): received = lax.all_to_all(message, 'dp', 0, 0, tiled=True)  10.3 us
    all_to_all x1, starting transfers between devices, per_device(): back = lax.all_to_all(both, FSDP, 0, 0, tiled=True)  6.3 us
  transfers between devices with their start and end apart: 4, of which 3 were waited for; matrix products, arithmetic and copies ran while one was open for 4% of the time, Pallas kernels for 0%

profile of v1, /device:TPU:2, one launch (start us, length us, event | category | flops | bytes accessed | tf_op | source)
XLA Modules:
  0.0 297.1 jit_solution(17274016032011043018)
XLA Ops:
  7.2 0.0 copy-start.4
  7.2 0.0 all-gather.3.cloned.1.call-start
  7.2 0.7 all-gather.3.cloned.1.call-update
  7.9 1.3 copy.30
  9.2 0.4 copy.25
  9.6 0.0 copy-done.4
  9.6 0.2 copy.26
  9.8 0.2 copy.27
  9.9 0.0 copy-start.5
  10.0 1.1 pad_maximum_fusion
  11.1 10.3 %all-to-all-start = ((bf16[8,576,128]{2,1,0:T(8,128)(2,1)}), bf16[8,576,128]{2,1,0:T(8,128)(2,1)S(1)}, u32[]{:S(2)}, u32[]{:S(2)}) async-start(bf16[8,576,128]{2,1,0:T(8,128)(2,1)} %pad_maximum_fusion), calls=%async_computation | async-start | bytes 2359296 | tf_op jit(solution)/shard_map/all_to_all | solution.py:29
  21.4 0.0 copy-done.5
  21.4 0.1 select_reduce_fusion
  21.5 0.1 fusion.9
  21.6 41.0 %all-to-all-done = bf16[8,576,128]{2,1,0:T(8,128)(2,1)S(1)} async-done(((bf16[8,576,128]{2,1,0:T(8,128)(2,1)}), bf16[8,576,128]{2,1,0:T(8,128)(2,1)S(1)}, u32[]{:S(2)}, u32[]{:S(2)}) %all-to-all-start) | async-done | bytes 1179680 | tf_op jit(solution)/shard_map/all_to_all | solution.py:29
  62.6 0.1 slice_reduce_fusion
  62.7 0.6 gather_fusion
  63.4 0.2 select_select_fusion
  63.6 22.2 %all_to_all.20 = bf16[64,16,128]{2,1,0:T(8,128)(2,1)S(1)} all-to-all(bf16[64,16,128]{2,1,0:T(8,128)(2,1)S(1)} %select_select_fusion), channel_id=1, replica_groups=mesh['fsdp_0'=4,'fsdp_1'=8,'fsdp_2'=2,'dp'=8] {'fsdp_0','fsdp_1','fsdp_2'}, dimensions={0} | all-to-all | bytes 524288 | tf_op jit(solution)/shard_map/all_to_all | solution.py:36
  85.8 0.0 all-gather.3.cloned.1.call-done
  85.8 1.6 stack.2
  87.4 3.6 %all-to-all-start.2 = ((bf16[8,1024,128]{2,1,0:T(8,128)(2,1)}), bf16[8,1024,128]{2,1,0:T(8,128)(2,1)S(1)}, u32[]{:S(2)}, u32[]{:S(2)}) async-start(bf16[8,1024,128]{2,1,0:T(8,128)(2,1)} %stack.2), calls=%async_computation.2 | async-start | bytes 4194304 | tf_op jit(solution)/shard_map/all_to_all | solution.py:39
  91.0 51.7 %all-to-all-done.2 = bf16[8,1024,128]{2,1,0:T(8,128)(2,1)S(1)} async-done(((bf16[8,1024,128]{2,1,0:T(8,128)(2,1)}), bf16[8,1024,128]{2,1,0:T(8,128)(2,1)S(1)}, u32[]{:S(2)}, u32[]{:S(2)}) %all-to-all-start.2) | async-done | bytes 2097184 | tf_op jit(solution)/shard_map/all_to_all | solution.py:39
  142.7 0.0 copy-start.1
  142.7 0.7 convolution_bitcast_fusion
  143.4 0.9 copy-done.1
  144.3 0.7 fusion.6
  145.0 1.4 fusion.2
  146.4 6.3 %all-to-all-start.3 = ((bf16[64,16,128]{2,1,0:T(8,128)(2,1)}), bf16[64,16,128]{2,1,0:T(8,128)(2,1)S(1)}, u32[]{:S(2)}, u32[]{:S(2)}) async-start(bf16[64,16,128]{2,1,0:T(8,128)(2,1)} %bitcast.14), calls=%async_computation.3 | async-start | bytes 524288 | tf_op jit(solution)/shard_map/all_to_all | solution.py:53
  152.7 0.0 copy-start.2
  152.7 2.6 copy.28
  155.3 0.0 copy-start
  155.3 0.0 copy-start.3
  155.3 0.0 copy-done.2
  155.3 3.1 %fusion = f32[1,128,1024]{2,1,0:T(8,128)} fusion(f32[1,128,1024]{2,1,0:T(8,128)S(1)} %copy-done.2, bf16[1024,1024]{0,1:T(8,128)(2,1)} %bitcast.46, s32[]{:T(128)S(6)} %select_n.60), kind=kOutput, calls=%fused_computation.8 | convolution fusion | flops 268566528 | bytes 3407876 | tf_op jit(solution)/shard_map/rc,kc->rk/dot_general | solution.py:56
  158.4 0.0 copy-done
  158.4 0.0 copy-done.3
  158.4 1.6 fusion.1
  160.1 4.2 %all-to-all-done.3 = bf16[64,16,128]{2,1,0:T(8,128)(2,1)S(1)} async-done(((bf16[64,16,128]{2,1,0:T(8,128)(2,1)}), bf16[64,16,128]{2,1,0:T(8,128)(2,1)S(1)}, u32[]{:S(2)}, u32[]{:S(2)}) %all-to-all-start.3) | async-done | bytes 262176 | tf_op jit(solution)/shard_map/all_to_all | solution.py:53
  164.2 0.6 multiply_reduce_fusion
  164.8 95.3 %psum.7 = f32[64]{0:T(128)S(1)} all-reduce(f32[64]{0:T(128)S(1)} %multiply_reduce_fusion), channel_id=1, replica_groups=mesh['fsdp_0'=4,'fsdp_1'=8,'fsdp_2'=2,'dp'=8] {'fsdp_0','fsdp_1','fsdp_2..., use_global_device_ids=true, to_apply=%region_4.5 | all-reduce | flops 64 | bytes 512 | tf_op jit(solution)/shard_map/psum | solution.py:63
  260.1 0.7 gather_fusion.2
  260.8 0.6 gather_fusion.1
  261.4 0.1 bitcast_select_fusion
  261.5 26.6 %all_gather.8 = bf16[8,28,16,128]{3,2,1,0:T(8,128)(2,1)S(1)} all-gather(bf16[1,28,16,128]{3,2,1,0:T(8,128)(2,1)S(1)} %bitcast_select_fusion), channel_id=1, replica_groups=mesh['fsdp_0'=4,'fsdp_1'=8,'fsdp_2'=2,'dp'=8] {'dp'}, dimensions={0}, use_global_device_ids=true | all-gather | bytes 1032192 | tf_op jit(solution)/shard_map/all_gather | solution.py:65
  288.1 0.3 fusion.3
  288.4 0.6 copy.29
  289.0 1.3 copy.33
  (6 shorter events, 0.0 us)
Async XLA Ops:
  7.2 2.4 copy-start.4
  7.2 78.6 %all-gather.3.cloned.1.call-start = ((), (), s32[]{:S(2)}) async-start(), calls=%async_computation.4 | async-start | bytes 2359296 | tf_op jit(solution)/shard_map/all_gather | solution.py:24
  9.9 11.4 %copy-start.5 = (s32[28]{0:T(128)S(1)}, s32[28]{0:T(128)}, u32[]{:S(2)}) copy-start(s32[28]{0:T(128)} %param.7) | copy-start | bytes 340
  11.1 51.5 %all-to-all-start = ((bf16[8,576,128]{2,1,0:T(8,128)(2,1)}), bf16[8,576,128]{2,1,0:T(8,128)(2,1)S(1)}, u32[]{:S(2)}, u32[]{:S(2)}) async-start(bf16[8,576,128]{2,1,0:T(8,128)(2,1)} %pad_maximum_fusion), calls=%async_computation | async-start | bytes 2359296 | tf_op jit(solution)/shard_map/all_to_all | solution.py:29
  87.4 55.3 %all-to-all-start.2 = ((bf16[8,1024,128]{2,1,0:T(8,128)(2,1)}), bf16[8,1024,128]{2,1,0:T(8,128)(2,1)S(1)}, u32[]{:S(2)}, u32[]{:S(2)}) async-start(bf16[8,1024,128]{2,1,0:T(8,128)(2,1)} %stack.2), calls=%async_computation.2 | async-start | bytes 4194304 | tf_op jit(solution)/shard_map/all_to_all | solution.py:39
  142.7 1.6 copy-start.1
  146.4 17.8 %all-to-all-start.3 = ((bf16[64,16,128]{2,1,0:T(8,128)(2,1)}), bf16[64,16,128]{2,1,0:T(8,128)(2,1)S(1)}, u32[]{:S(2)}, u32[]{:S(2)}) async-start(bf16[64,16,128]{2,1,0:T(8,128)(2,1)} %bitcast.14), calls=%async_computation.3 | async-start | bytes 524288 | tf_op jit(solution)/shard_map/all_to_all | solution.py:53
  152.7 2.6 copy-start.2
  155.3 3.1 %copy-start = (bf16[1024,8,128]{0,2,1:T(8,128)(2,1)S(1)}, bf16[1024,8,128]{0,2,1:T(8,128)(2,1)}, u32[]{:S(2)}) copy-start(bf16[1024,8,128]{0,2,1:T(8,128)(2,1)} %copy.28) | copy-start | bytes 6291460
  155.3 3.1 %copy-start.3 = (f32[1,128,1024]{2,1,0:T(8,128)S(1)}, f32[1,128,1024]{2,1,0:T(8,128)}, u32[]{:S(2)}) copy-start(f32[1,128,1024]{2,1,0:T(8,128)} %param.9) | copy-start | bytes 1572868
Sparse Core Ops, SparseCore 0:
  10.1 63.5 all-gather.2
